TPU v7x, 32 devices: a whole 2x2x4 slice. The times are simulated.
32 devices in a mesh: seq: 16 (over z, x, core), head: 2 (over y).
Axes of the slice: x: 2, y: 2, z: 4, core: 2. Of those that a mesh axis runs over, the one named last changes fastest.
Arguments:
- prompt_token_query: bfloat16 [512, 8192], P('seq', 'head'), may hold values from -6 to 6
- prompt_token_key: bfloat16 [512, 1024], P('seq', 'head'), may hold values from -6 to 6
- prompt_token_value: bfloat16 [512, 1024], P('seq', 'head'), may hold values from -6 to 6
- response_query_slots: bfloat16 [3072, 8192], P('seq', 'head'), may hold values from -160 to 160
- response_key_slots: bfloat16 [3072, 1024], P('seq', 'head'), may hold values from -6 to 6
- response_value_slots: bfloat16 [3072, 1024], P('seq', 'head'), may hold values from -6 to 6
- lengths: int32 [4], replicated, may hold values from 1 to 8, 16 in all
- block_table: int32 [16], replicated, may hold values from 0 to 15, each once
Outputs:
- prompt_out: bfloat16 [512, 8192], P(('seq', 'head'))
- answer_out: bfloat16 [3072, 8192], P(('seq', 'head'))
Inputs may be any that keep to these rules, and one draw needn't show every extreme that they name: `lengths`: they sum to 16; the largest is exactly 8. `block_table`: A permutation of 0 to 15.
All inputs are finite; a program needn't handle non-finite values.
Results may differ from a plain program's by a relative error of at most 0.007.
Values may be sent and summed in bfloat16 or wider, within the bound.
A program may use at most 64 MiB of HBM per device.

v0:
```python
import math
import jax
import jax.numpy as jnp
from jax import lax
from jax.sharding import PartitionSpec as P

HEAD_SIZE = 128
RESPONSE_BLOCK = 192
NEG_FILL = -1e30


def block_roles(lengths, global_blocks):
    bounds = jnp.cumsum(lengths)
    member = jnp.sum((global_blocks[:, None] >= bounds[None, :]).astype(jnp.int32), axis=1)
    starts = bounds - lengths
    owner_match = member[:, None] == jnp.arange(lengths.shape[0], dtype=jnp.int32)[None, :]
    first_block = jnp.sum(jnp.where(owner_match, starts[None, :], 0), axis=1)
    return (member, global_blocks - first_block, first_block)


def empty_state(row_count, heads_kv, query_group_width):
    peak_value = jnp.full((row_count, heads_kv, query_group_width), NEG_FILL, jnp.float32)
    weight_total = jnp.zeros((row_count, heads_kv, query_group_width), jnp.float32)
    mixed_sum = jnp.zeros((row_count, heads_kv, query_group_width, HEAD_SIZE), jnp.float32)
    return (peak_value, weight_total, mixed_sum)


def score_block(query_matrix, key_rows):
    return jnp.einsum(
        "rjgd,sjd->rjgs", query_matrix, key_rows, preferred_element_type=jnp.float32
    ) * HEAD_SIZE ** (-0.5)


def absorb(softmax_state, scores, visible, value_rows):
    peak_old, total_old, mixed_old = softmax_state
    masked = jnp.where(visible, scores, NEG_FILL)
    peak_new = jnp.maximum(peak_old, jnp.max(masked, axis=-1))
    factor = jnp.exp(peak_old - peak_new)
    weights = jnp.where(visible, jnp.exp(scores - peak_new[..., None]), 0.0)
    total_new = total_old * factor + jnp.sum(weights, axis=-1)
    mixed_new = mixed_old * factor[..., None] + jnp.einsum(
        "rjgs,sjd->rjgd",
        weights.astype(jnp.bfloat16),
        value_rows,
        preferred_element_type=jnp.float32,
    )
    return (peak_new, total_new, mixed_new)


def finish(softmax_state):
    peak_value, weight_total, mixed_sum = softmax_state
    row_count = mixed_sum.shape[0]
    return (mixed_sum / weight_total[..., None]).astype(jnp.bfloat16).reshape(row_count, -1)


def on_device(
    prompt_token_query,
    prompt_token_key,
    prompt_token_value,
    response_query_slots,
    response_key_slots,
    response_value_slots,
    lengths,
    block_table,
):
    heads_kv = response_key_slots.shape[1] // HEAD_SIZE
    heads_query = response_query_slots.shape[1] // HEAD_SIZE
    query_group_width = heads_query // heads_kv
    shard_rows = response_query_slots.shape[0]
    slot_count = shard_rows // RESPONSE_BLOCK
    prompt_rows = prompt_token_query.shape[0]
    most_blocks = block_table.shape[0] // 2
    batch_blocks = 4
    seq_place = lax.axis_index("seq")
    own_blocks = lax.dynamic_slice_in_dim(block_table, seq_place * slot_count, slot_count, 0)
    own_member, own_position, unused_first = block_roles(lengths, own_blocks)
    answer_queries = response_query_slots.reshape(
        slot_count, RESPONSE_BLOCK, heads_kv, query_group_width, HEAD_SIZE
    )
    prompt_queries = prompt_token_query.reshape(prompt_rows, heads_kv, query_group_width, HEAD_SIZE)
    prompt_positions = seq_place * prompt_rows + jnp.arange(prompt_rows, dtype=jnp.int32)
    initial = (
        tuple(
            (
                empty_state(RESPONSE_BLOCK, heads_kv, query_group_width)
                for slot_ordinal in range(slot_count)
            )
        ),
        empty_state(prompt_rows, heads_kv, query_group_width),
    )
    carried = initial
    piece_key = lax.all_gather(prompt_token_key, "seq", axis=0, tiled=True)
    piece_value = lax.all_gather(prompt_token_value, "seq", axis=0, tiled=True)
    row_count = piece_key.shape[0]
    part_width = math.gcd(row_count, prompt_rows * max(1, 256 // prompt_rows))
    part_count = row_count // part_width
    key_parts = piece_key.reshape(part_count, part_width, heads_kv, HEAD_SIZE)
    value_parts = piece_value.reshape(part_count, part_width, heads_kv, HEAD_SIZE)
    offsets = jnp.arange(part_count, dtype=jnp.int32) * part_width

    def one_part(state_in, part_data):
        key_rows, value_rows, offset = part_data
        answer_states, prompt_state = state_in
        all_seen = jnp.ones((1, 1, 1, part_width), dtype=bool)
        answer_states = tuple(
            (
                absorb(
                    answer_states[slot_ordinal],
                    score_block(answer_queries[slot_ordinal], key_rows),
                    all_seen,
                    value_rows,
                )
                for slot_ordinal in range(slot_count)
            )
        )
        key_positions = offset + jnp.arange(part_width, dtype=jnp.int32)
        seen = (key_positions[None, :] <= prompt_positions[:, None])[:, None, None, :]
        prompt_state = absorb(prompt_state, score_block(prompt_queries, key_rows), seen, value_rows)
        return ((answer_states, prompt_state), None)

    carried, unused_out = lax.scan(one_part, carried, (key_parts, value_parts, offsets))
    finished = carried
    piece_key = lax.all_gather(response_key_slots, "seq", axis=0, tiled=True)
    piece_value = lax.all_gather(response_value_slots, "seq", axis=0, tiled=True)
    block_total = piece_key.shape[0] // RESPONSE_BLOCK
    batch_count = -(-min(most_blocks, block_total) // batch_blocks)
    picked_total = batch_count * batch_blocks
    blocked_keys = piece_key.reshape(block_total, RESPONSE_BLOCK, heads_kv, HEAD_SIZE)
    blocked_values = piece_value.reshape(block_total, RESPONSE_BLOCK, heads_kv, HEAD_SIZE)
    piece_member, piece_position, unused_start = block_roles(lengths, block_table)
    block_ids = jnp.arange(block_total, dtype=jnp.int32)
    answer_states, prompt_state = finished
    slot_ordinal = 0
    wanted = (piece_member == own_member[slot_ordinal]) & (
        piece_position <= own_position[slot_ordinal]
    )
    ranking = jnp.cumsum(wanted.astype(jnp.int32)) - 1
    matches = wanted[None, :] & (
        ranking[None, :] == jnp.arange(picked_total, dtype=jnp.int32)[:, None]
    )
    chosen = jnp.sum(jnp.where(matches, block_ids[None, :], 0), axis=1)
    chosen_live = jnp.any(matches, axis=1)
    chosen_start = piece_position[chosen] * RESPONSE_BLOCK
    query_positions = own_position[slot_ordinal] * RESPONSE_BLOCK + jnp.arange(
        RESPONSE_BLOCK, dtype=jnp.int32
    )
    query_matrix = answer_queries[slot_ordinal]

    def one_batch(state_in, batch_data, query_matrix=query_matrix, query_positions=query_positions):
        picked, live_flags, starts_of = batch_data

        def take_in(state_now):
            key_rows = jnp.take(blocked_keys, picked, axis=0).reshape(
                batch_blocks * RESPONSE_BLOCK, heads_kv, HEAD_SIZE
            )
            value_rows = jnp.take(blocked_values, picked, axis=0).reshape(
                batch_blocks * RESPONSE_BLOCK, heads_kv, HEAD_SIZE
            )
            key_positions = (
                starts_of[:, None] + jnp.arange(RESPONSE_BLOCK, dtype=jnp.int32)[None, :]
            ).reshape(-1)
            key_live = jnp.repeat(live_flags, RESPONSE_BLOCK)
            seen = (key_live[None, :] & (key_positions[None, :] <= query_positions[:, None]))[
                :, None, None, :
            ]
            return absorb(state_now, score_block(query_matrix, key_rows), seen, value_rows)

        def keep_state(state_now):
            return state_now

        return (lax.cond(jnp.any(live_flags), take_in, keep_state, state_in), None)

    batch_inputs = (
        chosen.reshape(batch_count, batch_blocks),
        chosen_live.reshape(batch_count, batch_blocks),
        chosen_start.reshape(batch_count, batch_blocks),
    )
    new_state, unused_out = lax.scan(one_batch, answer_states[slot_ordinal], batch_inputs)
    updated = [new_state]
    finished = (tuple(updated), prompt_state)
    answer_states, prompt_state = finished
    answer_rows = jnp.concatenate([finish(state_item) for state_item in answer_states], axis=0)
    prompt_result = finish(prompt_state)
    prompt_out, answer_out = (
        lax.all_to_all(prompt_result, "head", split_axis=0, concat_axis=1, tiled=True),
        lax.all_to_all(answer_rows, "head", split_axis=0, concat_axis=1, tiled=True),
    )
    return (prompt_out, answer_out)


def solution(mesh):
    in_specs = (
        P("seq", "head"),
        P("seq", "head"),
        P("seq", "head"),
        P("seq", "head"),
        P("seq", "head"),
        P("seq", "head"),
        P(),
        P(),
    )
    out_specs = (P(("seq", "head"), None), P(("seq", "head"), None))
    return jax.shard_map(
        on_device, mesh=mesh, in_specs=in_specs, out_specs=out_specs, check_vma=False
    )
```

profile of v0, /device:TPU:1, one launch (start us, length us, event | category | flops | bytes accessed | tf_op | source)
XLA Modules:
  0.0 202.9 jit_solution(6942071327549159299)
XLA Ops:
  9.8 26.5 %all_gather.12 = bf16[512,512]{1,0:T(8,128)(2,1)} all-gather(bf16[32,512]{1,0:T(8,128)(2,1)} %param.17), channel_id=1, replica_groups=mesh['seq'=16,'head'=2] {'seq'}, dimensions={0}, use_global_device_ids=true | all-gather | bytes 557056 | tf_op jit(solution)/shard_map/all_gather | solution.py:92
  38.4 22.9 %all_gather.13 = bf16[512,512]{1,0:T(8,128)(2,1)} all-gather(bf16[32,512]{1,0:T(8,128)(2,1)} %param.18), channel_id=1, replica_groups=mesh['seq'=16,'head'=2] {'seq'}, dimensions={0}, use_global_device_ids=true | all-gather | bytes 557056 | tf_op jit(solution)/shard_map/all_gather | solution.py:93
  63.2 21.0 %while.37 = (s32[]{:T(128)}, f32[192,4,8]{0,2,1:T(8,128)S(1)}, f32[192,4,8]{0,2,1:T(8,128)S(1)}, f32[192,4,8,128]{3,0,2,1:T(8,128)S(1)}, f32[32,4,8]{0,2,1:T(8,1...) while((s32[]{:T(128)}, f32[192,4,8]{0,2,1:T(8,128)S(1)}, ...), condition=%wide.region_5.6_spmd.clone, body=%wide.region_0.5_spmd.clone.sunk | while | flops 957263104 | bytes 47417864 | solution.py:121
  71.4 2.3 %bitcast_add_fusion.3 = f32[192,4,8,128]{3,0,2,1:T(8,128)S(1)} fusion(f32[192,4,8,128]{3,0,2,1:T(8,128)S(1)} %get-tuple-element.658, f32[4,256,192,8]{1,2,3,0:T(8,128)S(1)} %get-tuple-element.626, f32[192,4,8]{0,2,1:T(8,128)S(1)} %select_maximum_fusion.4, f32[192,4,8]{0,2,1:T(8,128)S(1)} %get-tuple-element.628, pred[]{:T(512)S(6)} %compare.3, ...), kind=kOutput, calls=%fused_computation.11.clone.1 | convolution fusion | flops 409731072 | bytes 12894209 | tf_op jit(solution)/shard_map/while/body/eval_jaxpr/rjgs,sjd->rjgd/dot_general | solution.py:41
  81.9 2.3 %bitcast_add_fusion.3 = f32[192,4,8,128]{3,0,2,1:T(8,128)S(1)} fusion(f32[192,4,8,128]{3,0,2,1:T(8,128)S(1)} %get-tuple-element.658, f32[4,256,192,8]{1,2,3,0:T(8,128)S(1)} %get-tuple-element.626, f32[192,4,8]{0,2,1:T(8,128)S(1)} %select_maximum_fusion.4, f32[192,4,8]{0,2,1:T(8,128)S(1)} %get-tuple-element.628, pred[]{:T(512)S(6)} %compare.3, ...), kind=kOutput, calls=%fused_computation.11.clone.1 | convolution fusion | flops 409731072 | bytes 12894209 | tf_op jit(solution)/shard_map/while/body/eval_jaxpr/rjgs,sjd->rjgd/dot_general | solution.py:41
  88.0 4.3 %all-to-all-start = ((bf16[2,16,4096]{2,1,0:T(8,128)(2,1)}), bf16[2,16,4096]{2,1,0:T(8,128)(2,1)}, u32[]{:S(2)}, u32[]{:S(2)}) async-start(bf16[2,16,4096]{2,1,0:T(8,128)(2,1)} %all_to_all.28), calls=%async_computation | async-start | bytes 524288 | tf_op jit(solution)/shard_map/all_to_all | solution.py:185
  102.7 5.5 %reshape.241 = bf16[16,192,4,128]{3,2,1,0:T(4,128)(2,1)} reshape(bf16[3072,512]{1,0:T(8,128)(2,1)} %all-gather.3.cloned.1.call-done) | data formatting | bytes 6291456 | tf_op jit(solution)/shard_map/reshape | solution.py:128
  108.2 5.5 %reshape.242 = bf16[16,192,4,128]{3,2,1,0:T(4,128)(2,1)} reshape(bf16[3072,512]{1,0:T(8,128)(2,1)} %all-gather.5.cloned.1.call-done) | data formatting | bytes 6291456 | tf_op jit(solution)/shard_map/reshape | solution.py:129
  113.7 62.2 %while.36 = (s32[]{:T(128)}, f32[192,4,8]{0,2,1:T(8,128)S(1)}, f32[192,4,8]{0,2,1:T(8,128)S(1)}, f32[192,4,8,128]{3,0,2,1:T(8,128)S(1)}, pred[2,4]{1,0:T(4,128)(...) while((s32[]{:T(128)}, f32[192,4,8]{0,2,1:T(8,128)S(1)}, ...), condition=%wide.region_20.22_spmd.clone, body=%wide.region_14.21_spmd.clone.sunk | while | flops 2470492160 | bytes 155146736 | solution.py:178
  115.2 29.7 %conditional.3 = ((f32[192,4,8]{0,2,1:T(8,128)S(1)}, f32[192,4,8]{0,2,1:T(8,128)S(1)}, f32[192,4,8,128]{3,0,2,1:T(8,128)S(1)})) conditional(s32[]{:T(128)} %convert_element_type.62, (f32[192,4,8]{0,2,1:T(8,128)S(1)}, f32[192,4,8]{0,2,1:T(8,128)S(1)}, f32[192,4,8,128]{3,0,2,1:T(8,128)S(1)}) %tuple.83, (pred[1,4]{1,0:T(4,128)(4,1)S(1)}, ...), branch_computations={%region_16.16_spmd, %region_17.20_spmd} | conditional | flops 2470492160 | bytes 155145696 | solution.py:171
  115.5 3.9 %gather_fusion.1 = bf16[4,192,4,128]{3,2,1,0:T(4,128)(2,1)} fusion(bf16[16,192,4,128]{3,2,1,0:T(4,128)(2,1)} %get-tuple-element.205, s32[1024]{0:T(1024)S(1)} %pad_clamp_fusion), kind=kCustom, calls=%fused_computation.1.clone | custom fusion | bytes 1572880 | tf_op jit(solution)/shard_map/while/body/eval_jaxpr/cond/branch_1_fun/jit(_take)/gather | solution.py:156
  119.5 4.0 %gather_fusion = bf16[4,192,4,128]{3,2,1,0:T(4,128)(2,1)} fusion(bf16[16,192,4,128]{3,2,1,0:T(4,128)(2,1)} %get-tuple-element.200, s32[1024]{0:T(1024)S(1)} %pad_clamp_fusion), kind=kCustom, calls=%fused_computation.clone | custom fusion | bytes 1572880 | tf_op jit(solution)/shard_map/while/body/eval_jaxpr/cond/branch_1_fun/jit(_take)/gather | solution.py:153
  125.8 3.5 %fusion.27 = (f32[192,4,8]{0,2,1:T(8,128)S(1)}, f32[4,768,192,8]{1,2,3,0:T(8,128)S(1)}) fusion(pred[192,768]{1,0:T(8,128)(4,1)S(1)} %compare_and_fusion, bf16[192,4,8,128]{3,0,2,1:T(8,128)(2,1)S(1)} %copy-done.2, bf16[768,4,128,1]{2,1,0,3:T(4,128)(2,1)S(1)} %bitcast.130), kind=kOutput, calls=%fused_computation.48 | convolution fusion | flops 1222109184 | bytes 21405696 | tf_op jit(solution)/shard_map/while/body/eval_jaxpr/cond/branch_1_fun/rjgd,sjd->rjgs/dot_general | solution.py:29
  129.4 5.4 %fusion.31 = f32[192,4,8]{0,2,1:T(8,128)S(1)} fusion(f32[4,768,192,8]{1,2,3,0:T(8,128)S(1)} %get-tuple-element.457, f32[192,4,8]{0,2,1:T(8,128)S(1)} %max.10, pred[192,768]{1,0:T(8,128)(4,1)S(1)} %compare_and_fusion), kind=kLoop, calls=%fused_computation.52 | loop fusion | flops 18868224 | bytes 19070976 | tf_op jit(solution)/shard_map/while/body/eval_jaxpr/cond/branch_1_fun/reduce_sum | solution.py:40
  135.9 9.0 %bitcast_add_fusion.1 = f32[192,4,8,128]{3,0,2,1:T(8,128)S(1)} fusion(f32[192,4,8,128]{3,0,2,1:T(8,128)S(1)} %get-tuple-element.204, f32[4,768,192,8]{1,2,3,0:T(8,128)} %copy-done, f32[192,4,8]{0,2,1:T(8,128)S(1)} %max.10, pred[192,768]{1,0:T(8,128)(4,1)S(1)} %compare_and_fusion, f32[192,4,8]{0,2,1:T(8,128)S(1)} %get-tuple-element.438, ...), kind=kOutput, calls=%fused_computation.55 | convolution fusion | flops 1228406784 | bytes 26148864 | tf_op jit(solution)/shard_map/while/body/eval_jaxpr/cond/branch_1_fun/rjgs,sjd->rjgd/dot_general | solution.py:41
  146.3 29.7 %conditional.3 = ((f32[192,4,8]{0,2,1:T(8,128)S(1)}, f32[192,4,8]{0,2,1:T(8,128)S(1)}, f32[192,4,8,128]{3,0,2,1:T(8,128)S(1)})) conditional(s32[]{:T(128)} %convert_element_type.62, (f32[192,4,8]{0,2,1:T(8,128)S(1)}, f32[192,4,8]{0,2,1:T(8,128)S(1)}, f32[192,4,8,128]{3,0,2,1:T(8,128)S(1)}) %tuple.83, (pred[1,4]{1,0:T(4,128)(4,1)S(1)}, ...), branch_computations={%region_16.16_spmd, %region_17.20_spmd} | conditional | flops 2470492160 | bytes 155145696 | solution.py:171
  146.7 3.9 %gather_fusion.1 = bf16[4,192,4,128]{3,2,1,0:T(4,128)(2,1)} fusion(bf16[16,192,4,128]{3,2,1,0:T(4,128)(2,1)} %get-tuple-element.205, s32[1024]{0:T(1024)S(1)} %pad_clamp_fusion), kind=kCustom, calls=%fused_computation.1.clone | custom fusion | bytes 1572880 | tf_op jit(solution)/shard_map/while/body/eval_jaxpr/cond/branch_1_fun/jit(_take)/gather | solution.py:156
  150.6 4.0 %gather_fusion = bf16[4,192,4,128]{3,2,1,0:T(4,128)(2,1)} fusion(bf16[16,192,4,128]{3,2,1,0:T(4,128)(2,1)} %get-tuple-element.200, s32[1024]{0:T(1024)S(1)} %pad_clamp_fusion), kind=kCustom, calls=%fused_computation.clone | custom fusion | bytes 1572880 | tf_op jit(solution)/shard_map/while/body/eval_jaxpr/cond/branch_1_fun/jit(_take)/gather | solution.py:153
  154.6 2.2 %broadcast_select_fusion = (bf16[4,192,4,128]{3,2,1,0:T(4,128)(2,1)S(1)}, bf16[4,192,4,128]{3,2,1,0:T(4,128)(2,1)S(1)}) fusion(bf16[4,192,4,128]{3,2,1,0:T(4,128)(2,1)} %gather_fusion.1, pred[4]{0:T(512)(128)(4,1)S(1)} %get-tuple-element.439, bf16[4,192,4,128]{3,2,1,0:T(4,128)(2,1)} %gather_fusion), kind=kLoop, calls=%fused_computation.59 | loop fusion | flops 786432 | bytes 3145732 | tf_op jit(solution)/shard_map/while/body/eval_jaxpr/cond/branch_1_fun/jit(_take)/select_n | solution.py:156
  157.0 3.5 %fusion.27 = (f32[192,4,8]{0,2,1:T(8,128)S(1)}, f32[4,768,192,8]{1,2,3,0:T(8,128)S(1)}) fusion(pred[192,768]{1,0:T(8,128)(4,1)S(1)} %compare_and_fusion, bf16[192,4,8,128]{3,0,2,1:T(8,128)(2,1)S(1)} %copy-done.2, bf16[768,4,128,1]{2,1,0,3:T(4,128)(2,1)S(1)} %bitcast.130), kind=kOutput, calls=%fused_computation.48 | convolution fusion | flops 1222109184 | bytes 21405696 | tf_op jit(solution)/shard_map/while/body/eval_jaxpr/cond/branch_1_fun/rjgd,sjd->rjgs/dot_general | solution.py:29
  160.5 5.4 %fusion.31 = f32[192,4,8]{0,2,1:T(8,128)S(1)} fusion(f32[4,768,192,8]{1,2,3,0:T(8,128)S(1)} %get-tuple-element.457, f32[192,4,8]{0,2,1:T(8,128)S(1)} %max.10, pred[192,768]{1,0:T(8,128)(4,1)S(1)} %compare_and_fusion), kind=kLoop, calls=%fused_computation.52 | loop fusion | flops 18868224 | bytes 19070976 | tf_op jit(solution)/shard_map/while/body/eval_jaxpr/cond/branch_1_fun/reduce_sum | solution.py:40
  167.0 9.0 %bitcast_add_fusion.1 = f32[192,4,8,128]{3,0,2,1:T(8,128)S(1)} fusion(f32[192,4,8,128]{3,0,2,1:T(8,128)S(1)} %get-tuple-element.204, f32[4,768,192,8]{1,2,3,0:T(8,128)} %copy-done, f32[192,4,8]{0,2,1:T(8,128)S(1)} %max.10, pred[192,768]{1,0:T(8,128)(4,1)S(1)} %compare_and_fusion, f32[192,4,8]{0,2,1:T(8,128)S(1)} %get-tuple-element.438, ...), kind=kOutput, calls=%fused_computation.55 | convolution fusion | flops 1228406784 | bytes 26148864 | tf_op jit(solution)/shard_map/while/body/eval_jaxpr/cond/branch_1_fun/rjgs,sjd->rjgd/dot_general | solution.py:41
  180.1 3.7 %all-to-all-start.1 = ((bf16[2,96,4096]{2,1,0:T(8,128)(2,1)}), bf16[2,96,4096]{2,1,0:T(8,128)(2,1)S(1)}, u32[]{:S(2)}, u32[]{:S(2)}) async-start(bf16[2,96,4096]{2,1,0:T(8,128)(2,1)} %all_to_all.32), calls=%async_computation.1 | async-start | bytes 3145728 | tf_op jit(solution)/shard_map/all_to_all | solution.py:186
  185.4 9.4 %all-to-all-done.1 = bf16[2,96,4096]{2,1,0:T(8,128)(2,1)S(1)} async-done(((bf16[2,96,4096]{2,1,0:T(8,128)(2,1)}), bf16[2,96,4096]{2,1,0:T(8,128)(2,1)S(1)}, u32[]{:S(2)}, u32[]{:S(2)}) %all-to-all-start.1) | async-done | bytes 1572896 | tf_op jit(solution)/shard_map/all_to_all | solution.py:186
  (134 shorter events, 49.5 us)
Async XLA Ops:
  7.2 95.5 %all-gather.3.cloned.1.call-start = ((), (), s32[]{:S(2)}) async-start(), calls=%async_computation.2 | async-start | bytes 3342336 | tf_op jit(solution)/shard_map/all_gather | solution.py:123
  7.9 100.3 %all-gather.5.cloned.1.call-start = ((), (), s32[]{:S(2)}) async-start(), calls=%async_computation.3 | async-start | bytes 3342336 | tf_op jit(solution)/shard_map/all_gather | solution.py:124
  63.2 29.1 %copy-start.5 = (s32[4]{0:T(128)S(1)}, s32[4]{0:T(128)}, u32[]{:S(2)}) copy-start(s32[4]{0:T(128)} %param.22) | copy-start | bytes 52
  63.2 29.3 %copy-start.6 = (s32[16]{0:T(128)S(1)}, s32[16]{0:T(128)}, u32[]{:S(2)}) copy-start(s32[16]{0:T(128)} %param.23) | copy-start | bytes 196
  63.2 3.4 %copy-start.3 = (f32[32,4,8,128]{3,0,2,1:T(8,128)S(1)}, f32[32,4,8,128]{3,0,2,1:T(8,128)}, u32[]{:S(2)}) copy-start(f32[32,4,8,128]{3,0,2,1:T(8,128)} %get-tuple-element.661) | copy-start | bytes 1572868 | tf_op jit(solution)/shard_map/while
  64.5 2.7 %copy-start.1 = (bf16[192,4096]{1,0:T(8,128)(2,1)S(1)}, bf16[192,4096]{1,0:T(8,128)(2,1)}, u32[]{:S(2)}) copy-start(bf16[192,4096]{1,0:T(8,128)(2,1)} %get-tuple-element.678) | copy-start | bytes 4718596 | tf_op jit(solution)/shard_map/while
  67.1 2.0 copy-start.4
  73.7 3.4 %copy-start.3 = (f32[32,4,8,128]{3,0,2,1:T(8,128)S(1)}, f32[32,4,8,128]{3,0,2,1:T(8,128)}, u32[]{:S(2)}) copy-start(f32[32,4,8,128]{3,0,2,1:T(8,128)} %get-tuple-element.661) | copy-start | bytes 1572868 | tf_op jit(solution)/shard_map/while
  75.0 2.7 %copy-start.1 = (bf16[192,4096]{1,0:T(8,128)(2,1)S(1)}, bf16[192,4096]{1,0:T(8,128)(2,1)}, u32[]{:S(2)}) copy-start(bf16[192,4096]{1,0:T(8,128)(2,1)} %get-tuple-element.678) | copy-start | bytes 4718596 | tf_op jit(solution)/shard_map/while
  77.6 2.0 copy-start.4
  88.0 92.1 %all-to-all-start = ((bf16[2,16,4096]{2,1,0:T(8,128)(2,1)}), bf16[2,16,4096]{2,1,0:T(8,128)(2,1)}, u32[]{:S(2)}, u32[]{:S(2)}) async-start(bf16[2,16,4096]{2,1,0:T(8,128)(2,1)} %all_to_all.28), calls=%async_computation | async-start | bytes 524288 | tf_op jit(solution)/shard_map/all_to_all | solution.py:185
  123.4 2.4 %copy-start.2 = (bf16[192,4,8,128]{3,0,2,1:T(8,128)(2,1)S(1)}, bf16[192,4,8,128]{3,0,2,1:T(8,128)(2,1)}, u32[]{:S(2)}) copy-start(bf16[192,4,8,128]{3,0,2,1:T(8,128)(2,1)} %get-tuple-element.202) | copy-start | bytes 4718596 | tf_op jit(solution)/shard_map/while/body/eval_jaxpr/cond
  129.4 6.5 %copy-start = (f32[4,768,192,8]{1,2,3,0:T(8,128)}, f32[4,768,192,8]{1,2,3,0:T(8,128)S(1)}, u32[]{:S(2)}) copy-start(f32[4,768,192,8]{1,2,3,0:T(8,128)S(1)} %get-tuple-element.457) | copy-start | bytes 56623108 | tf_op jit(solution)/shard_map/while/body/eval_jaxpr/cond
  154.6 2.4 %copy-start.2 = (bf16[192,4,8,128]{3,0,2,1:T(8,128)(2,1)S(1)}, bf16[192,4,8,128]{3,0,2,1:T(8,128)(2,1)}, u32[]{:S(2)}) copy-start(bf16[192,4,8,128]{3,0,2,1:T(8,128)(2,1)} %get-tuple-element.202) | copy-start | bytes 4718596 | tf_op jit(solution)/shard_map/while/body/eval_jaxpr/cond
  160.5 6.5 %copy-start = (f32[4,768,192,8]{1,2,3,0:T(8,128)}, f32[4,768,192,8]{1,2,3,0:T(8,128)S(1)}, u32[]{:S(2)}) copy-start(f32[4,768,192,8]{1,2,3,0:T(8,128)S(1)} %get-tuple-element.457) | copy-start | bytes 56623108 | tf_op jit(solution)/shard_map/while/body/eval_jaxpr/cond
  180.1 14.7 %all-to-all-start.1 = ((bf16[2,96,4096]{2,1,0:T(8,128)(2,1)}), bf16[2,96,4096]{2,1,0:T(8,128)(2,1)S(1)}, u32[]{:S(2)}, u32[]{:S(2)}) async-start(bf16[2,96,4096]{2,1,0:T(8,128)(2,1)} %all_to_all.32), calls=%async_computation.1 | async-start | bytes 3145728 | tf_op jit(solution)/shard_map/all_to_all | solution.py:186
Sparse Core Ops, SparseCore 0:
  10.3 50.5 all-gather.2
  63.2 44.9 all-gather.4
where the time goes:
time: 204 us; the launch traced here: 203 us
  local copies, waits for them, and re-layouts  52.9 us (26%)
  blocking collectives  49.4 us (24%)
  matrix products  34.5 us (17%)
  other arithmetic  30.1 us (15%)
  between operations  15.4 us (8%)
  waiting for transfers between devices  10.7 us (5%)
  starting transfers between devices  8.04 us (4%)
    all_gather x1, blocking collectives, on_device(): piece_key = lax.all_gather(prompt_token_key, 'seq', axis=0, tiled=True)  26.5 us
    dot_general x6, matrix products, absorb(): jnp.einsum('rjgs,sjd->rjgd', weights.astype(jnp.bfloat16), value_rows, pr...  23.4 us
    all_gather x1, blocking collectives, on_device(): piece_value = lax.all_gather(prompt_token_value, 'seq', axis=0, tiled=True)  22.9 us
    reduce_sum x6, other arithmetic, absorb(): total_new = total_old * factor + jnp.sum(weights, axis=-1)  15.9 us
    dot_general x6, matrix products, score_block(): jnp.einsum('rjgd,sjd->rjgs', query_matrix, key_rows, preferred_element_ty...  11 us
    all_to_all x1, waiting for transfers between devices, on_device(): lax.all_to_all(answer_rows, 'head', split_axis=0, concat_axis=1, tiled=True)  9.36 us
    gather x2, local copies, waits for them, and re-layouts, take_in(): jnp.take(blocked_keys, picked, axis=0)  7.93 us
    gather x2, local copies, waits for them, and re-layouts, take_in(): jnp.take(blocked_values, picked, axis=0)  7.87 us
  transfers between devices with their start and end apart: 4, of which 1 were waited for; matrix products, arithmetic and copies ran while one was open for 54% of the time, Pallas kernels for 0%

commit v1 on v0

--- a/solution.py
+++ b/solution.py
@@ -89,8 +89,16 @@
         empty_state(prompt_rows, heads_kv, query_group_width),
     )
     carried = initial
-    piece_key = lax.all_gather(prompt_token_key, "seq", axis=0, tiled=True)
-    piece_value = lax.all_gather(prompt_token_value, "seq", axis=0, tiled=True)
+    piece_key, piece_value = jnp.split(
+        lax.all_gather(
+            jnp.concatenate([prompt_token_key, prompt_token_value], axis=1),
+            "seq",
+            axis=0,
+            tiled=True,
+        ),
+        [prompt_token_key.shape[1]],
+        axis=1,
+    )
     row_count = piece_key.shape[0]
     part_width = math.gcd(row_count, prompt_rows * max(1, 256 // prompt_rows))
     part_count = row_count // part_width

time: 204 us -> 240 us (1.18)
  waiting for transfers between devices: 10.7 us -> 88.8 us
  blocking collectives: 49.4 us -> 0 us
  other arithmetic: 30.1 us -> 34.4 us
  local copies, waits for them, and re-layouts: 52.9 us -> 55.8 us
    all_gather x2 -> x0, blocking collectives: 49.4 us -> none  [the longest x1 26.5 us: on_device(): piece_key = lax.all_gather(prompt_token_key, 'seq', axis=0, tiled=True)]
    all_gather x1, waiting for transfers between devices: 0.01 us -> 40.7 us  [on_device(): lax.all_gather(response_value_slots, 'seq', axis=0, tiled=True)]
    all_gather x0 -> x1, waiting for transfers between devices: none -> 26.1 us  [on_device(): lax.all_gather(jnp.concatenate([prompt_token_key, prompt_token_value], ax...]
    all_gather x1, waiting for transfers between devices: 0.01 us -> 11.2 us  [on_device(): piece_key = lax.all_gather(response_key_slots, 'seq', axis=0, tiled=True)]
  transfers between devices with their start and end apart: 4 -> 5, of which waited for: 1 -> 4; matrix products, arithmetic and copies ran while one was open for 54% -> 49% of each run, Pallas kernels for 0% -> 0%
where the time goes in v1:
time: 240 us; the launch traced here: 238 us
  waiting for transfers between devices  88.8 us (37%)
  local copies, waits for them, and re-layouts  55.8 us (23%)
  matrix products  34.5 us (14%)
  other arithmetic  34.4 us (14%)
  between operations  15.1 us (6%)
  starting transfers between devices  8.08 us (3%)
    all_gather x1, waiting for transfers between devices, on_device(): lax.all_gather(response_value_slots, 'seq', axis=0, tiled=True)  40.7 us
    all_gather x1, waiting for transfers between devices, on_device(): lax.all_gather(jnp.concatenate([prompt_token_key, prompt_token_value], ax...  26.1 us
    dot_general x6, matrix products, absorb(): jnp.einsum('rjgs,sjd->rjgd', weights.astype(jnp.bfloat16), value_rows, pr...  23.4 us
    reduce_sum x6, other arithmetic, absorb(): total_new = total_old * factor + jnp.sum(weights, axis=-1)  15.9 us
    all_gather x1, waiting for transfers between devices, on_device(): piece_key = lax.all_gather(response_key_slots, 'seq', axis=0, tiled=True)  11.2 us
    dot_general x6, matrix products, score_block(): jnp.einsum('rjgd,sjd->rjgs', query_matrix, key_rows, preferred_element_ty...  11 us
    all_to_all x1, waiting for transfers between devices, on_device(): lax.all_to_all(answer_rows, 'head', split_axis=0, concat_axis=1, tiled=True)  9.36 us
    gather x2, local copies, waits for them, and re-layouts, take_in(): jnp.take(blocked_keys, picked, axis=0)  7.93 us
  transfers between devices with their start and end apart: 5, of which 4 were waited for; matrix products, arithmetic and copies ran while one was open for 49% of the time, Pallas kernels for 0%

profile of v1, /device:TPU:1, one launch (start us, length us, event | category | flops | bytes accessed | tf_op | source)
XLA Modules:
  0.0 238.4 jit_solution(11931580740484169831)
XLA Ops:
  25.0 26.1 %all-gather.4.cloned.1.call-done = bf16[512,1024]{1,0:T(8,128)(2,1)} async-done(((bf16[32,1024]{1,0:T(8,128)(2,1)}), bf16[512,1024]{1,0:T(8,128)(2,1)}) %all-gather.4.cloned.1.call-update) | async-done | bytes 1048592 | tf_op jit(solution)/shard_map/all_gather | solution.py:93
  51.1 2.3 fusion.48
  57.4 21.1 %while.37 = (s32[]{:T(128)}, f32[192,4,8]{0,2,1:T(8,128)S(1)}, f32[192,4,8]{0,2,1:T(8,128)S(1)}, f32[192,4,8,128]{3,0,2,1:T(8,128)S(1)}, f32[32,4,8]{0,2,1:T(8,1...) while((s32[]{:T(128)}, f32[192,4,8]{0,2,1:T(8,128)S(1)}, ...), condition=%wide.region_5.6_spmd.clone, body=%wide.region_0.5_spmd.clone.sunk | while | flops 957263104 | bytes 47417864 | solution.py:129
  65.6 2.3 bitcast_add_fusion.3
  82.4 4.3 %all-to-all-start = ((bf16[2,16,4096]{2,1,0:T(8,128)(2,1)}), bf16[2,16,4096]{2,1,0:T(8,128)(2,1)}, u32[]{:S(2)}, u32[]{:S(2)}) async-start(bf16[2,16,4096]{2,1,0:T(8,128)(2,1)} %all_to_all.28), calls=%async_computation | async-start | bytes 524288 | tf_op jit(solution)/shard_map/all_to_all | solution.py:193
  86.7 11.2 %all-gather.6.cloned.1.call-done = bf16[3072,512]{1,0:T(8,128)(2,1)} async-done(((bf16[192,512]{1,0:T(8,128)(2,1)}), bf16[3072,512]{1,0:T(8,128)(2,1)}) %all-gather.6.cloned.1.call-update) | async-done | bytes 3145744 | tf_op jit(solution)/shard_map/all_gather | solution.py:131
  97.8 5.5 %reshape.241 = bf16[16,192,4,128]{3,2,1,0:T(4,128)(2,1)} reshape(bf16[3072,512]{1,0:T(8,128)(2,1)} %all-gather.6.cloned.1.call-done) | data formatting | bytes 6291456 | tf_op jit(solution)/shard_map/reshape | solution.py:136
  103.3 40.7 %all-gather.8.cloned.1.call-done = bf16[3072,512]{1,0:T(8,128)(2,1)} async-done(((bf16[192,512]{1,0:T(8,128)(2,1)}), bf16[3072,512]{1,0:T(8,128)(2,1)}) %all-gather.8.cloned.1.call-update) | async-done | bytes 3145744 | tf_op jit(solution)/shard_map/all_gather | solution.py:132
  144.0 5.5 %reshape.242 = bf16[16,192,4,128]{3,2,1,0:T(4,128)(2,1)} reshape(bf16[3072,512]{1,0:T(8,128)(2,1)} %all-gather.8.cloned.1.call-done) | data formatting | bytes 6291456 | tf_op jit(solution)/shard_map/reshape | solution.py:137
  149.5 62.2 %while.36 = (s32[]{:T(128)}, f32[192,4,8]{0,2,1:T(8,128)S(1)}, f32[192,4,8]{0,2,1:T(8,128)S(1)}, f32[192,4,8,128]{3,0,2,1:T(8,128)S(1)}, pred[2,4]{1,0:T(4,128)(...) while((s32[]{:T(128)}, f32[192,4,8]{0,2,1:T(8,128)S(1)}, ...), condition=%wide.region_20.22_spmd.clone, body=%wide.region_14.21_spmd.clone.sunk | while | flops 2470492160 | bytes 155146736 | solution.py:186
  151.0 29.7 %conditional.3 = ((f32[192,4,8]{0,2,1:T(8,128)S(1)}, f32[192,4,8]{0,2,1:T(8,128)S(1)}, f32[192,4,8,128]{3,0,2,1:T(8,128)S(1)})) conditional(s32[]{:T(128)} %convert_element_type.62, (f32[192,4,8]{0,2,1:T(8,128)S(1)}, f32[192,4,8]{0,2,1:T(8,128)S(1)}, f32[192,4,8,128]{3,0,2,1:T(8,128)S(1)}) %tuple.84, (pred[1,4]{1,0:T(4,128)(4,1)S(1)}, ...), branch_computations={%region_16.16_spmd, %region_17.20_spmd} | conditional | flops 2470492160 | bytes 155145696 | solution.py:179
  151.3 3.9 %gather_fusion.1 = bf16[4,192,4,128]{3,2,1,0:T(4,128)(2,1)} fusion(bf16[16,192,4,128]{3,2,1,0:T(4,128)(2,1)} %get-tuple-element.205, s32[1024]{0:T(1024)S(1)} %pad_clamp_fusion), kind=kCustom, calls=%fused_computation.1.clone | custom fusion | bytes 1572880 | tf_op jit(solution)/shard_map/while/body/eval_jaxpr/cond/branch_1_fun/jit(_take)/gather | solution.py:164
  155.3 4.0 %gather_fusion = bf16[4,192,4,128]{3,2,1,0:T(4,128)(2,1)} fusion(bf16[16,192,4,128]{3,2,1,0:T(4,128)(2,1)} %get-tuple-element.200, s32[1024]{0:T(1024)S(1)} %pad_clamp_fusion), kind=kCustom, calls=%fused_computation.clone | custom fusion | bytes 1572880 | tf_op jit(solution)/shard_map/while/body/eval_jaxpr/cond/branch_1_fun/jit(_take)/gather | solution.py:161
  161.6 3.5 %fusion.27 = (f32[192,4,8]{0,2,1:T(8,128)S(1)}, f32[4,768,192,8]{1,2,3,0:T(8,128)S(1)}) fusion(pred[192,768]{1,0:T(8,128)(4,1)S(1)} %compare_and_fusion, bf16[192,4,8,128]{3,0,2,1:T(8,128)(2,1)S(1)} %copy-done.2, bf16[768,4,128,1]{2,1,0,3:T(4,128)(2,1)S(1)} %bitcast.130), kind=kOutput, calls=%fused_computation.48 | convolution fusion | flops 1222109184 | bytes 21405696 | tf_op jit(solution)/shard_map/while/body/eval_jaxpr/cond/branch_1_fun/rjgd,sjd->rjgs/dot_general | solution.py:29
  165.2 5.4 %fusion.31 = f32[192,4,8]{0,2,1:T(8,128)S(1)} fusion(f32[4,768,192,8]{1,2,3,0:T(8,128)S(1)} %get-tuple-element.457, f32[192,4,8]{0,2,1:T(8,128)S(1)} %max.10, pred[192,768]{1,0:T(8,128)(4,1)S(1)} %compare_and_fusion), kind=kLoop, calls=%fused_computation.52 | loop fusion | flops 18868224 | bytes 19070976 | tf_op jit(solution)/shard_map/while/body/eval_jaxpr/cond/branch_1_fun/reduce_sum | solution.py:40
  171.7 9.0 %bitcast_add_fusion.1 = f32[192,4,8,128]{3,0,2,1:T(8,128)S(1)} fusion(f32[192,4,8,128]{3,0,2,1:T(8,128)S(1)} %get-tuple-element.204, f32[4,768,192,8]{1,2,3,0:T(8,128)} %copy-done, f32[192,4,8]{0,2,1:T(8,128)S(1)} %max.10, pred[192,768]{1,0:T(8,128)(4,1)S(1)} %compare_and_fusion, f32[192,4,8]{0,2,1:T(8,128)S(1)} %get-tuple-element.438, ...), kind=kOutput, calls=%fused_computation.55 | convolution fusion | flops 1228406784 | bytes 26148864 | tf_op jit(solution)/shard_map/while/body/eval_jaxpr/cond/branch_1_fun/rjgs,sjd->rjgd/dot_general | solution.py:41
  182.1 29.7 %conditional.3 = ((f32[192,4,8]{0,2,1:T(8,128)S(1)}, f32[192,4,8]{0,2,1:T(8,128)S(1)}, f32[192,4,8,128]{3,0,2,1:T(8,128)S(1)})) conditional(s32[]{:T(128)} %convert_element_type.62, (f32[192,4,8]{0,2,1:T(8,128)S(1)}, f32[192,4,8]{0,2,1:T(8,128)S(1)}, f32[192,4,8,128]{3,0,2,1:T(8,128)S(1)}) %tuple.84, (pred[1,4]{1,0:T(4,128)(4,1)S(1)}, ...), branch_computations={%region_16.16_spmd, %region_17.20_spmd} | conditional | flops 2470492160 | bytes 155145696 | solution.py:179
  182.5 3.9 %gather_fusion.1 = bf16[4,192,4,128]{3,2,1,0:T(4,128)(2,1)} fusion(bf16[16,192,4,128]{3,2,1,0:T(4,128)(2,1)} %get-tuple-element.205, s32[1024]{0:T(1024)S(1)} %pad_clamp_fusion), kind=kCustom, calls=%fused_computation.1.clone | custom fusion | bytes 1572880 | tf_op jit(solution)/shard_map/while/body/eval_jaxpr/cond/branch_1_fun/jit(_take)/gather | solution.py:164
  186.4 4.0 %gather_fusion = bf16[4,192,4,128]{3,2,1,0:T(4,128)(2,1)} fusion(bf16[16,192,4,128]{3,2,1,0:T(4,128)(2,1)} %get-tuple-element.200, s32[1024]{0:T(1024)S(1)} %pad_clamp_fusion), kind=kCustom, calls=%fused_computation.clone | custom fusion | bytes 1572880 | tf_op jit(solution)/shard_map/while/body/eval_jaxpr/cond/branch_1_fun/jit(_take)/gather | solution.py:161
  192.8 3.5 %fusion.27 = (f32[192,4,8]{0,2,1:T(8,128)S(1)}, f32[4,768,192,8]{1,2,3,0:T(8,128)S(1)}) fusion(pred[192,768]{1,0:T(8,128)(4,1)S(1)} %compare_and_fusion, bf16[192,4,8,128]{3,0,2,1:T(8,128)(2,1)S(1)} %copy-done.2, bf16[768,4,128,1]{2,1,0,3:T(4,128)(2,1)S(1)} %bitcast.130), kind=kOutput, calls=%fused_computation.48 | convolution fusion | flops 1222109184 | bytes 21405696 | tf_op jit(solution)/shard_map/while/body/eval_jaxpr/cond/branch_1_fun/rjgd,sjd->rjgs/dot_general | solution.py:29
  196.3 5.4 %fusion.31 = f32[192,4,8]{0,2,1:T(8,128)S(1)} fusion(f32[4,768,192,8]{1,2,3,0:T(8,128)S(1)} %get-tuple-element.457, f32[192,4,8]{0,2,1:T(8,128)S(1)} %max.10, pred[192,768]{1,0:T(8,128)(4,1)S(1)} %compare_and_fusion), kind=kLoop, calls=%fused_computation.52 | loop fusion | flops 18868224 | bytes 19070976 | tf_op jit(solution)/shard_map/while/body/eval_jaxpr/cond/branch_1_fun/reduce_sum | solution.py:40
  202.8 9.0 %bitcast_add_fusion.1 = f32[192,4,8,128]{3,0,2,1:T(8,128)S(1)} fusion(f32[192,4,8,128]{3,0,2,1:T(8,128)S(1)} %get-tuple-element.204, f32[4,768,192,8]{1,2,3,0:T(8,128)} %copy-done, f32[192,4,8]{0,2,1:T(8,128)S(1)} %max.10, pred[192,768]{1,0:T(8,128)(4,1)S(1)} %compare_and_fusion, f32[192,4,8]{0,2,1:T(8,128)S(1)} %get-tuple-element.438, ...), kind=kOutput, calls=%fused_computation.55 | convolution fusion | flops 1228406784 | bytes 26148864 | tf_op jit(solution)/shard_map/while/body/eval_jaxpr/cond/branch_1_fun/rjgs,sjd->rjgd/dot_general | solution.py:41
  215.9 3.7 %all-to-all-start.1 = ((bf16[2,96,4096]{2,1,0:T(8,128)(2,1)}), bf16[2,96,4096]{2,1,0:T(8,128)(2,1)S(1)}, u32[]{:S(2)}, u32[]{:S(2)}) async-start(bf16[2,96,4096]{2,1,0:T(8,128)(2,1)} %all_to_all.32), calls=%async_computation.1 | async-start | bytes 3145728 | tf_op jit(solution)/shard_map/all_to_all | solution.py:194
  221.2 9.4 %all-to-all-done.1 = bf16[2,96,4096]{2,1,0:T(8,128)(2,1)S(1)} async-done(((bf16[2,96,4096]{2,1,0:T(8,128)(2,1)}), bf16[2,96,4096]{2,1,0:T(8,128)(2,1)S(1)}, u32[]{:S(2)}, u32[]{:S(2)}) %all-to-all-start.1) | async-done | bytes 1572896 | tf_op jit(solution)/shard_map/all_to_all | solution.py:194
  (133 shorter events, 59.0 us)
Async XLA Ops:
  7.2 44.0 %all-gather.4.cloned.1.call-start = ((), (), s32[]{:S(2)}) async-start(), calls=%async_computation.2 | async-start | bytes 1114112 | tf_op jit(solution)/shard_map/all_gather | solution.py:93
  8.6 89.2 %all-gather.6.cloned.1.call-start = ((), (), s32[]{:S(2)}) async-start(), calls=%async_computation.3 | async-start | bytes 3342336 | tf_op jit(solution)/shard_map/all_gather | solution.py:131
  9.4 134.6 %all-gather.8.cloned.1.call-start = ((), (), s32[]{:S(2)}) async-start(), calls=%async_computation.4 | async-start | bytes 3342336 | tf_op jit(solution)/shard_map/all_gather | solution.py:132
  57.4 3.5 %copy-start.3 = (f32[32,4,8,128]{3,0,2,1:T(8,128)S(1)}, f32[32,4,8,128]{3,0,2,1:T(8,128)}, u32[]{:S(2)}) copy-start(f32[32,4,8,128]{3,0,2,1:T(8,128)} %get-tuple-element.663) | copy-start | bytes 1572868 | tf_op jit(solution)/shard_map/while
  58.7 2.7 %copy-start.1 = (bf16[192,4096]{1,0:T(8,128)(2,1)S(1)}, bf16[192,4096]{1,0:T(8,128)(2,1)}, u32[]{:S(2)}) copy-start(bf16[192,4096]{1,0:T(8,128)(2,1)} %get-tuple-element.680) | copy-start | bytes 4718596 | tf_op jit(solution)/shard_map/while
  61.4 2.0 copy-start.4
  68.0 3.5 %copy-start.3 = (f32[32,4,8,128]{3,0,2,1:T(8,128)S(1)}, f32[32,4,8,128]{3,0,2,1:T(8,128)}, u32[]{:S(2)}) copy-start(f32[32,4,8,128]{3,0,2,1:T(8,128)} %get-tuple-element.663) | copy-start | bytes 1572868 | tf_op jit(solution)/shard_map/while
  69.3 2.7 %copy-start.1 = (bf16[192,4096]{1,0:T(8,128)(2,1)S(1)}, bf16[192,4096]{1,0:T(8,128)(2,1)}, u32[]{:S(2)}) copy-start(bf16[192,4096]{1,0:T(8,128)(2,1)} %get-tuple-element.680) | copy-start | bytes 4718596 | tf_op jit(solution)/shard_map/while
  72.0 2.0 copy-start.4
  82.4 133.5 %all-to-all-start = ((bf16[2,16,4096]{2,1,0:T(8,128)(2,1)}), bf16[2,16,4096]{2,1,0:T(8,128)(2,1)}, u32[]{:S(2)}, u32[]{:S(2)}) async-start(bf16[2,16,4096]{2,1,0:T(8,128)(2,1)} %all_to_all.28), calls=%async_computation | async-start | bytes 524288 | tf_op jit(solution)/shard_map/all_to_all | solution.py:193
  159.2 2.4 %copy-start.2 = (bf16[192,4,8,128]{3,0,2,1:T(8,128)(2,1)S(1)}, bf16[192,4,8,128]{3,0,2,1:T(8,128)(2,1)}, u32[]{:S(2)}) copy-start(bf16[192,4,8,128]{3,0,2,1:T(8,128)(2,1)} %get-tuple-element.202) | copy-start | bytes 4718596 | tf_op jit(solution)/shard_map/while/body/eval_jaxpr/cond
  165.2 6.5 %copy-start = (f32[4,768,192,8]{1,2,3,0:T(8,128)}, f32[4,768,192,8]{1,2,3,0:T(8,128)S(1)}, u32[]{:S(2)}) copy-start(f32[4,768,192,8]{1,2,3,0:T(8,128)S(1)} %get-tuple-element.457) | copy-start | bytes 56623108 | tf_op jit(solution)/shard_map/while/body/eval_jaxpr/cond
  190.4 2.4 %copy-start.2 = (bf16[192,4,8,128]{3,0,2,1:T(8,128)(2,1)S(1)}, bf16[192,4,8,128]{3,0,2,1:T(8,128)(2,1)}, u32[]{:S(2)}) copy-start(bf16[192,4,8,128]{3,0,2,1:T(8,128)(2,1)} %get-tuple-element.202) | copy-start | bytes 4718596 | tf_op jit(solution)/shard_map/while/body/eval_jaxpr/cond
  196.3 6.5 %copy-start = (f32[4,768,192,8]{1,2,3,0:T(8,128)}, f32[4,768,192,8]{1,2,3,0:T(8,128)S(1)}, u32[]{:S(2)}) copy-start(f32[4,768,192,8]{1,2,3,0:T(8,128)S(1)} %get-tuple-element.457) | copy-start | bytes 56623108 | tf_op jit(solution)/shard_map/while/body/eval_jaxpr/cond
  215.9 14.7 %all-to-all-start.1 = ((bf16[2,96,4096]{2,1,0:T(8,128)(2,1)}), bf16[2,96,4096]{2,1,0:T(8,128)(2,1)S(1)}, u32[]{:S(2)}, u32[]{:S(2)}) async-start(bf16[2,96,4096]{2,1,0:T(8,128)(2,1)} %all_to_all.32), calls=%async_computation.1 | async-start | bytes 3145728 | tf_op jit(solution)/shard_map/all_to_all | solution.py:194
Sparse Core Ops, SparseCore 0:
  10.7 40.3 all-gather.3
  53.4 44.4 all-gather.5
  100.1 43.8 all-gather.7
